TPU v7x, 512 devices: a whole 4x4x16 slice. The times are simulated.
512 devices in a mesh: obs: 16 (over x, y), patch: 32 (over z, core).
Axes of the slice: x: 4, y: 4, z: 16, core: 2. Of those that a mesh axis runs over, the one named last changes fastest.
Arguments:
- green: float32 [20480, 20480], P('obs', 'patch'), may hold values from -0.0390625 to 0.0390625
- data: float32 [20480, 128], P('obs'), may hold values from -6 to 6
- neighbours: int32 [3, 20480], P(None, 'patch'), may hold values from 0 to 20479, as said below
- reg_weight: float32 [128], replicated, may hold values from 0.5 to 2
Outputs:
- slip: float32 [20480, 128], P('patch')
Inputs may be any that keep to these rules, and one draw needn't show every extreme that they name: `neighbours`: entry (k, i) is a patch within 128 of i; an entry equal to i is padding. Distance 128 is reached in every draw.
All inputs are finite; a program needn't handle non-finite values.
Results may differ from a plain program's by a relative error of at most 0.0001.
Values sent between devices are 32-bit elements; how exact they have to be, the bound alone decides.
A program may use at most 64 MiB of HBM per device.

v0:
```python
import jax
import jax.numpy as jnp
from jax import lax
from jax.sharding import Mesh
from jax.sharding import PartitionSpec as P

BAND = 128
ITERS = 3
PATCH = ("patch_0", "patch_1")
OBS = ("obs_0", "obs_1")
OBS_PATCH = ("obs_0", "obs_1", "patch_0", "patch_1")


def extended_2(shard, sides, width):
    for axis, dim in sides:
        size, length = (lax.axis_size(axis), shard.shape[dim])
        up = [(i, (i + 1) % size) for i in range(size - 1)]
        down = [(j, i) for i, j in up]
        last = lax.slice_in_dim(shard, length - width, length, axis=dim)
        first = lax.slice_in_dim(shard, 0, width, axis=dim)
        before = lax.ppermute(last, axis, up)
        after = lax.ppermute(first, axis, down)
        shard = jnp.concatenate([before, shard, after], axis=dim)
    return shard


def shifted(value, axis, steps):
    count = lax.axis_size(axis)
    first, last = (max(0, -steps), min(count, count - steps))
    return lax.ppermute(value, axis, [(source, source + steps) for source in range(first, last)])


def cut_along(shard, dim, length):
    before, after = (shard.shape[:dim], shard.shape[dim + 1 :])
    return jnp.moveaxis(shard.reshape(*before, length, -1, *after), dim, 0)


def summed_on_arrival(shard, axis, dim):
    length = lax.axis_size(axis)
    pieces = lax.all_to_all(cut_along(shard, dim, length), axis, 0, 0, tiled=True)
    return jnp.sum(pieces, axis=0)


def joined_along(pieces, dim):
    dims = list(pieces.shape[1:])
    dims[dim] *= pieces.shape[0]
    return jnp.moveaxis(pieces, 0, dim).reshape(dims)


def all_blocks(shard, axes, sequence):
    pieces = shard[None]
    for k in sequence:
        pieces = lax.all_gather(pieces, axes[k], axis=0, tiled=True)
    block = [lax.axis_size(axes[k]) for k in reversed(sequence)]
    pieces = pieces.reshape(*block, *shard.shape)
    turned = sorted(range(len(sequence)), key=lambda place: sequence[len(sequence) - 1 - place])
    return pieces.transpose(*turned, *range(len(sequence), pieces.ndim)).reshape(-1, *shard.shape)


def gather_axes(shard, axes, sequence, dim):
    return joined_along(all_blocks(shard, axes, sequence), dim)


def total_of_pieces(shard, axis):
    pieces = lax.all_gather(shard, axis)
    return pieces.sum(axis=0)


def sent_to_all(shard, axis):
    length = lax.axis_size(axis)
    return lax.all_to_all(
        jnp.broadcast_to(shard[None], (length, *shard.shape)), axis, 0, 0, tiled=True
    )


def taken_together(shard, axis):
    everything = sent_to_all(shard, axis)
    return jnp.sum(everything, axis=0)


def over_axes_2(shard, axes):
    for axis in axes:
        shard = lax.psum(shard, axis)
    return shard


def back_product(block, residual):
    return lax.dot_general(
        block,
        residual,
        (((0,), (0,)), ((), ())),
        precision=lax.Precision.HIGHEST,
        preferred_element_type=jnp.float32,
    )


def shards(green, data, neighbours, reg_weight):
    highest = lax.Precision.HIGHEST
    row_count, col_count = green.shape
    epochs = data.shape[1]
    n_patch = lax.axis_size(PATCH)
    offset = lax.axis_index(PATCH) * col_count
    local_ids = neighbours - offset + BAND
    obs_first = lax.axis_index(OBS) == 0
    share = row_count // n_patch
    residual = lax.dynamic_slice_in_dim(data, lax.axis_index(PATCH) * share, share, 0)

    def back_partial(residual):
        return back_product(green, gather_axes(residual, PATCH, (0, 1), 0))

    def gradient_of(residual):
        return total_of_pieces(back_partial(residual), OBS)

    def squared_norm(gradient):
        return taken_together(jnp.sum(gradient * gradient, axis=0), PATCH)

    slip = jnp.zeros((col_count, epochs), jnp.float32)
    reg_resid = jnp.zeros((col_count, epochs), jnp.float32)
    gradient = gradient_of(residual)
    grad_norm = squared_norm(gradient)
    direction = gradient
    for iteration in range(ITERS):
        image = summed_on_arrival(
            jnp.dot(green, direction, precision=highest, preferred_element_type=jnp.float32),
            PATCH,
            0,
        )
        image, image_sq = (image, jnp.sum(image * image, axis=0))
        extended = extended_2(direction, ((PATCH, 0),), BAND)
        reg_image = reg_weight * (
            4.0 * direction
            - extended[local_ids[0]]
            - extended[local_ids[1]]
            - extended[local_ids[2]]
        )
        reg_sq = jnp.where(obs_first, jnp.sum(reg_image * reg_image, axis=0), 0.0)
        curvature = over_axes_2(image_sq + reg_sq, OBS_PATCH)
        step_size = grad_norm / curvature
        slip = slip + step_size * direction
        if iteration + 1 < ITERS:
            residual = residual - step_size * image
            reg_resid = reg_resid - step_size * reg_image
            spread = jnp.zeros((col_count + 2 * BAND, epochs), jnp.float32)
            for slot in range(3):
                spread = spread.at[local_ids[slot]].add(reg_resid)
            from_left = shifted(spread[BAND + col_count :], PATCH, 1)
            from_right = shifted(spread[:BAND], PATCH, -1)
            filler = jnp.zeros((col_count - BAND, epochs), jnp.float32)
            inside = (
                spread[BAND : BAND + col_count]
                + jnp.concatenate([from_left, filler], 0)
                + jnp.concatenate([filler, from_right], 0)
            )
            gradient = gradient_of(residual) + reg_weight * (4.0 * reg_resid - inside)
            next_norm = squared_norm(gradient)
            direction = gradient + next_norm / grad_norm * direction
            grad_norm = next_norm
    return slip


def solution(mesh):
    split = Mesh(mesh.devices.reshape(4, 4, 16, 2), ("obs_0", "obs_1", "patch_0", "patch_1"))
    in_specs = (P(OBS, PATCH), P(OBS, None), P(None, PATCH), P())
    out_specs = P(PATCH, None)
    return jax.shard_map(
        shards, mesh=split, in_specs=in_specs, out_specs=out_specs, check_vma=False
    )
```

profile of v0, /device:TPU:1, one launch (start us, length us, event | category | flops | bytes accessed | tf_op | source)
XLA Modules:
  0.0 751.9 jit_solution(1936652341242088612)
XLA Ops:
  7.4 30.9 %all-gather = f32[640,128]{1,0:T(8,128)S(1)} all-gather(f32[40,128]{1,0:T(8,128)S(1)} %constant_dynamic-slice_fusion), channel_id=2, replica_groups=mesh['obs_0'=4,'obs_1'=4,'patch_0'=16,'patch_1'=2] {'patch_0'}, dimensions={0}, use_global_device_ids=true | all-gather | bytes 348160 | tf_op jit(solution)/shard_map/all_gather | solution.py:53
  38.3 9.9 %all_gather.37 = f32[32,40,128]{2,1,0:T(8,128)S(1)} all-gather(f32[16,40,128]{2,1,0:T(8,128)S(1)} %bitcast.84), channel_id=1, replica_groups=mesh['obs_0'=4,'obs_1'=4,'patch_0'=16,'patch_1'=2] {'patch_1'}, dimensions={0}, use_global_device_ids=true | all-gather | bytes 983040 | tf_op jit(solution)/shard_map/all_gather | solution.py:53
  51.3 67.2 %all-gather.10.cloned.1.call-done = f32[10240,128]{0,1:T(8,128)} async-done(((f32[640,128]{0,1:T(8,128)}), f32[10240,128]{0,1:T(8,128)}) %all-gather.10.cloned.1.call-update) | async-done | bytes 5242896 | tf_op jit(solution)/shard_map/all_gather | solution.py:65
  118.4 3.4 copy.59
  124.1 13.2 %all-to-all-start = ((f32[32,1,128]{2,1,0:T(1,128)}), f32[32,1,128]{2,1,0:T(1,128)S(1)}, u32[]{:S(2)}, u32[]{:S(2)}) async-start(f32[32,1,128]{2,1,0:T(1,128)} %broadcast_in_dim.21), calls=%async_computation | async-start | bytes 32768 | tf_op jit(solution)/shard_map/all_to_all | solution.py:71
  137.3 5.3 convolution_bitcast_fusion.2
  144.8 4.3 all-to-all-done
  149.1 7.9 %all-to-all-start.1 = ((f32[32,40,128]{2,1,0:T(8,128)}), f32[32,40,128]{2,1,0:T(8,128)}, u32[]{:S(2)}, u32[]{:S(2)}) async-start(f32[32,40,128]{2,1,0:T(8,128)} %bitcast.75), calls=%async_computation.1 | async-start | bytes 1310720 | tf_op jit(solution)/shard_map/all_to_all | solution.py:40
  160.5 3.5 collective-permute-start
  166.0 16.8 %collective-permute-done = f32[128,128]{1,0:T(8,128)S(1)} collective-permute-done((f32[128,128]{1,0:T(8,128)}, f32[128,128]{1,0:T(8,128)S(1)}, u32[]{:S(2)}, u32[]{:S(2)}) %collective-permute-start) | collective-permute-done | bytes 65568 | tf_op jit(solution)/shard_map/ppermute | solution.py:21
  182.8 4.5 collective-permute-done.1
  202.1 8.4 %psum.84 = f32[128]{0:T(128)S(1)} all-reduce(f32[128]{0:T(128)S(1)} %fusion.23), channel_id=1, replica_groups=mesh['obs_0'=4,'obs_1'=4,'patch_0'=16,'patch_1'=2] {'obs_0'}, use_global_device_ids=true, to_apply=%region_6.7 | all-reduce | flops 128 | bytes 1024 | tf_op jit(solution)/shard_map/psum | solution.py:83
  210.5 6.5 psum.85
  217.0 24.1 %psum.86 = f32[128]{0:T(128)S(1)} all-reduce(f32[128]{0:T(128)S(1)} %psum.85), channel_id=1, replica_groups=mesh['obs_0'=4,'obs_1'=4,'patch_0'=16,'patch_1'=2] {'patch_0'}, use_global_device_ids=true, to_apply=%region_8.9 | all-reduce | flops 128 | bytes 1024 | tf_op jit(solution)/shard_map/psum | solution.py:83
  241.2 13.6 %psum.87 = f32[128]{0:T(128)S(1)} all-reduce(f32[128]{0:T(128)S(1)} %psum.86), channel_id=1, replica_groups=mesh['obs_0'=4,'obs_1'=4,'patch_0'=16,'patch_1'=2] {'patch_1'}, use_global_device_ids=true, to_apply=%region_9.10 | all-reduce | flops 128 | bytes 1024 | tf_op jit(solution)/shard_map/psum | solution.py:83
  255.5 21.6 %all-gather.2 = f32[640,128]{1,0:T(8,128)S(1)} all-gather(f32[40,128]{1,0:T(8,128)S(1)} %multiply_subtract_fusion.6), channel_id=4, replica_groups=mesh['obs_0'=4,'obs_1'=4,'patch_0'=16,'patch_1'=2] {'patch_0'}, dimensions={0}, use_global_device_ids=true | all-gather | bytes 348160 | tf_op jit(solution)/shard_map/all_gather | solution.py:53
  277.1 9.2 %all_gather.41 = f32[32,40,128]{2,1,0:T(8,128)S(1)} all-gather(f32[16,40,128]{2,1,0:T(8,128)S(1)} %bitcast.86), channel_id=1, replica_groups=mesh['obs_0'=4,'obs_1'=4,'patch_0'=16,'patch_1'=2] {'patch_1'}, dimensions={0}, use_global_device_ids=true | all-gather | bytes 983040 | tf_op jit(solution)/shard_map/all_gather | solution.py:53
  289.4 7.2 scatter_custom_fusion
  296.6 7.7 %scatter_custom_fusion.1 = f32[896,128]{1,0:T(8,128)} fusion(f32[896,128]{1,0:T(8,128)} %scatter_custom_fusion, s32[640]{0:T(1024)S(1)} %get-tuple-element.7, f32[640,128]{1,0:T(8,128)} %get-tuple-element.15, f32[]{:T(128)} %constant.8.clone.1, f32[128]{0:T(128)S(1)} %div.23), kind=kCustom, calls=%fused_computation.55 | custom fusion | flops 245760 | bytes 787456 | tf_op jit(solution)/shard_map/scatter-add | solution.py:145
  304.3 7.7 %scatter_custom_fusion.2 = f32[896,128]{1,0:T(8,128)} fusion(f32[896,128]{1,0:T(8,128)} %scatter_custom_fusion.1, s32[640]{0:T(1024)S(1)} %get-tuple-element.6, f32[640,128]{1,0:T(8,128)} %get-tuple-element.15, f32[]{:T(128)} %constant.8.clone.1, f32[128]{0:T(128)S(1)} %div.23), kind=kCustom, calls=%fused_computation.54 | custom fusion | flops 245760 | bytes 787456 | tf_op jit(solution)/shard_map/scatter-add | solution.py:145
  318.9 35.8 %all-gather.12.cloned.1.call-done = f32[10240,128]{0,1:T(8,128)} async-done(((f32[640,128]{0,1:T(8,128)}), f32[10240,128]{0,1:T(8,128)}) %all-gather.12.cloned.1.call-update) | async-done | bytes 5242896 | tf_op jit(solution)/shard_map/all_gather | solution.py:65
  363.5 24.8 %all_to_all.33 = f32[32,1,128]{2,1,0:T(1,128)S(1)} all-to-all(f32[32,1,128]{2,1,0:T(1,128)S(1)} %broadcast_in_dim.25), channel_id=1, replica_groups=mesh['obs_0'=4,'obs_1'=4,'patch_0'=16,'patch_1'=2] {'patch_0','patch_1'}, dimensions={0} | all-to-all | bytes 32768 | tf_op jit(solution)/shard_map/all_to_all | solution.py:71
  390.2 4.3 convolution_bitcast_fusion.1
  396.6 5.1 all-to-all-start.3
  402.7 3.5 collective-permute-start.4
  408.2 19.1 %collective-permute-done.4 = f32[128,128]{1,0:T(8,128)S(1)} collective-permute-done((f32[128,128]{1,0:T(8,128)S(1)}, f32[128,128]{1,0:T(8,128)S(1)}, u32[]{:S(2)}, u32[]{:S(2)}) %collective-permute-start.4) | collective-permute-done | bytes 65568 | tf_op jit(solution)/shard_map/ppermute | solution.py:21
  427.3 5.0 collective-permute-done.5
  447.1 8.4 %psum.88 = f32[128]{0:T(128)S(1)} all-reduce(f32[128]{0:T(128)S(1)} %fusion.24), channel_id=1, replica_groups=mesh['obs_0'=4,'obs_1'=4,'patch_0'=16,'patch_1'=2] {'obs_0'}, use_global_device_ids=true, to_apply=%region_19.20 | all-reduce | flops 128 | bytes 1024 | tf_op jit(solution)/shard_map/psum | solution.py:83
  455.5 6.5 psum.89
  462.0 23.9 %psum.90 = f32[128]{0:T(128)S(1)} all-reduce(f32[128]{0:T(128)S(1)} %psum.89), channel_id=1, replica_groups=mesh['obs_0'=4,'obs_1'=4,'patch_0'=16,'patch_1'=2] {'patch_0'}, use_global_device_ids=true, to_apply=%region_21.22 | all-reduce | flops 128 | bytes 1024 | tf_op jit(solution)/shard_map/psum | solution.py:83
  485.9 13.6 %psum.91 = f32[128]{0:T(128)S(1)} all-reduce(f32[128]{0:T(128)S(1)} %psum.90), channel_id=1, replica_groups=mesh['obs_0'=4,'obs_1'=4,'patch_0'=16,'patch_1'=2] {'patch_1'}, use_global_device_ids=true, to_apply=%region_22.23 | all-reduce | flops 128 | bytes 1024 | tf_op jit(solution)/shard_map/psum | solution.py:83
  499.5 21.6 %all-gather.4 = f32[640,128]{1,0:T(8,128)S(1)} all-gather(f32[40,128]{1,0:T(8,128)S(1)} %multiply_subtract_fusion.5), channel_id=6, replica_groups=mesh['obs_0'=4,'obs_1'=4,'patch_0'=16,'patch_1'=2] {'patch_0'}, dimensions={0}, use_global_device_ids=true | all-gather | bytes 348160 | tf_op jit(solution)/shard_map/all_gather | solution.py:53
  521.1 9.3 %all_gather.45 = f32[32,40,128]{2,1,0:T(8,128)S(1)} all-gather(f32[16,40,128]{2,1,0:T(8,128)S(1)} %bitcast.85), channel_id=1, replica_groups=mesh['obs_0'=4,'obs_1'=4,'patch_0'=16,'patch_1'=2] {'patch_1'}, dimensions={0}, use_global_device_ids=true | all-gather | bytes 983040 | tf_op jit(solution)/shard_map/all_gather | solution.py:53
  535.3 7.2 scatter_custom_fusion.3
  542.5 7.6 %scatter_fusion = f32[896,128]{1,0:T(8,128)} fusion(f32[896,128]{1,0:T(8,128)} %scatter_custom_fusion.3, s32[640]{0:T(1024)S(1)} %get-tuple-element.7, f32[640,128]{1,0:T(8,128)} %multiply_subtract_fusion), kind=kCustom, calls=%fused_computation.13 | custom fusion | flops 81920 | bytes 985600 | tf_op jit(solution)/shard_map/scatter-add | solution.py:145
  550.1 7.6 %scatter_fusion.1 = f32[896,128]{1,0:T(8,128)} fusion(f32[896,128]{1,0:T(8,128)} %scatter_fusion, s32[640]{0:T(1024)S(1)} %get-tuple-element.6, f32[640,128]{1,0:T(8,128)} %multiply_subtract_fusion), kind=kCustom, calls=%fused_computation.14 | custom fusion | flops 81920 | bytes 985600 | tf_op jit(solution)/shard_map/scatter-add | solution.py:145
  564.8 33.9 %all-gather.14.cloned.1.call-done = f32[10240,128]{0,1:T(8,128)} async-done(((f32[640,128]{0,1:T(8,128)}), f32[10240,128]{0,1:T(8,128)}) %all-gather.14.cloned.1.call-update) | async-done | bytes 5242896 | tf_op jit(solution)/shard_map/all_gather | solution.py:65
  598.7 3.4 copy.61
  607.6 24.8 %all_to_all.34 = f32[32,1,128]{2,1,0:T(1,128)S(1)} all-to-all(f32[32,1,128]{2,1,0:T(1,128)S(1)} %broadcast_in_dim.27), channel_id=1, replica_groups=mesh['obs_0'=4,'obs_1'=4,'patch_0'=16,'patch_1'=2] {'patch_0','patch_1'}, dimensions={0} | all-to-all | bytes 32768 | tf_op jit(solution)/shard_map/all_to_all | solution.py:71
  634.2 4.3 convolution_bitcast_fusion
  640.7 5.1 all-to-all-start.5
  646.7 3.5 collective-permute-start.8
  652.2 19.2 %collective-permute-done.8 = f32[128,128]{1,0:T(8,128)S(1)} collective-permute-done((f32[128,128]{1,0:T(8,128)S(1)}, f32[128,128]{1,0:T(8,128)S(1)}, u32[]{:S(2)}, u32[]{:S(2)}) %collective-permute-start.8) | collective-permute-done | bytes 65568 | tf_op jit(solution)/shard_map/ppermute | solution.py:21
  671.4 5.0 collective-permute-done.9
  690.5 8.4 %psum.92 = f32[128]{0:T(128)S(1)} all-reduce(f32[128]{0:T(128)S(1)} %fusion.25), channel_id=1, replica_groups=mesh['obs_0'=4,'obs_1'=4,'patch_0'=16,'patch_1'=2] {'obs_0'}, use_global_device_ids=true, to_apply=%region_32.33 | all-reduce | flops 128 | bytes 1024 | tf_op jit(solution)/shard_map/psum | solution.py:83
  698.9 6.8 psum.93
  705.6 23.7 %psum.94 = f32[128]{0:T(128)S(1)} all-reduce(f32[128]{0:T(128)S(1)} %psum.93), channel_id=1, replica_groups=mesh['obs_0'=4,'obs_1'=4,'patch_0'=16,'patch_1'=2] {'patch_0'}, use_global_device_ids=true, to_apply=%region_34.35 | all-reduce | flops 128 | bytes 1024 | tf_op jit(solution)/shard_map/psum | solution.py:83
  729.3 13.6 %psum.95 = f32[128]{0:T(128)S(1)} all-reduce(f32[128]{0:T(128)S(1)} %psum.94), channel_id=1, replica_groups=mesh['obs_0'=4,'obs_1'=4,'patch_0'=16,'patch_1'=2] {'patch_1'}, use_global_device_ids=true, to_apply=%region_35.36 | all-reduce | flops 128 | bytes 1024 | tf_op jit(solution)/shard_map/psum | solution.py:83
  (102 shorter events, 110.2 us)
Async XLA Ops:
  6.5 41.7 %copy-start = (f32[1280,640]{1,0:T(8,128)S(1)}, f32[1280,640]{1,0:T(8,128)}, u32[]{:S(2)}) copy-start(f32[1280,640]{1,0:T(8,128)} %param.4) | copy-start | bytes 9830404
  6.5 111.9 %all-gather.10.cloned.1.call-start = ((), (), s32[]{:S(2)}) async-start(), calls=%async_computation.6 | async-start | bytes 5570560 | tf_op jit(solution)/shard_map/all_gather | solution.py:65
  122.7 0.7 copy-start.3
  124.1 24.9 %all-to-all-start = ((f32[32,1,128]{2,1,0:T(1,128)}), f32[32,1,128]{2,1,0:T(1,128)S(1)}, u32[]{:S(2)}, u32[]{:S(2)}) async-start(f32[32,1,128]{2,1,0:T(1,128)} %broadcast_in_dim.21), calls=%async_computation | async-start | bytes 32768 | tf_op jit(solution)/shard_map/all_to_all | solution.py:71
  137.3 19.7 %copy-start.5 = (s32[3,640]{1,0:T(4,128)S(1)}, s32[3,640]{1,0:T(4,128)}, u32[]{:S(2)}) copy-start(s32[3,640]{1,0:T(4,128)} %param.6) | copy-start | bytes 23044
  149.1 51.8 %all-to-all-start.1 = ((f32[32,40,128]{2,1,0:T(8,128)}), f32[32,40,128]{2,1,0:T(8,128)}, u32[]{:S(2)}, u32[]{:S(2)}) async-start(f32[32,40,128]{2,1,0:T(8,128)} %bitcast.75), calls=%async_computation.1 | async-start | bytes 1310720 | tf_op jit(solution)/shard_map/all_to_all | solution.py:40
  157.0 197.6 %all-gather.12.cloned.1.call-start = ((), (), s32[]{:S(2)}) async-start(), calls=%async_computation.7 | async-start | bytes 5570560 | tf_op jit(solution)/shard_map/all_gather | solution.py:65
  160.5 22.3 %collective-permute-start = (f32[128,128]{1,0:T(8,128)}, f32[128,128]{1,0:T(8,128)S(1)}, u32[]{:S(2)}, u32[]{:S(2)}) collective-permute-start(f32[128,128]{1,0:T(8,128)} %get-tuple-element.24), channel_id=1, source_target_pairs={{0,1},{1,2},{2,3},{3,4},{4,5},{5,6},{6,7},{7,8},{8,9},{9,10},{10,1... | collective-permute-start | bytes 196616 | tf_op jit(solution)/shard_map/ppermute | solution.py:21
  164.1 23.2 %collective-permute-start.1 = (f32[128,128]{1,0:T(8,128)S(1)}, f32[128,128]{1,0:T(8,128)S(1)}, u32[]{:S(2)}, u32[]{:S(2)}) collective-permute-start(f32[128,128]{1,0:T(8,128)S(1)} %get-tuple-element.25), channel_id=1, source_target_pairs={{1,0},{2,1},{3,2},{4,3},{5,4},{6,5},{7,6},{8,7},{9,8},{10,9},{11,1... | collective-permute-start | bytes 196616 | tf_op jit(solution)/shard_map/ppermute | solution.py:22
  192.3 6.5 copy-start.4
  313.4 48.0 %collective-permute-start.2 = (f32[128,128]{1,0:T(8,128)}, f32[128,128]{1,0:T(8,128)S(1)}, u32[]{:S(2)}, u32[]{:S(2)}) collective-permute-start(f32[128,128]{1,0:T(8,128)} %get-tuple-element.18), channel_id=1, source_target_pairs={{0,1},{1,2},{2,3},{3,4},{4,5},{5,6},{6,7},{7,8},{8,9},{9,10},{10,1... | collective-permute-start | bytes 196616 | tf_op jit(solution)/shard_map/ppermute | solution.py:30
  316.7 44.8 %collective-permute-start.3 = (f32[128,128]{1,0:T(8,128)S(1)}, f32[128,128]{1,0:T(8,128)S(1)}, u32[]{:S(2)}, u32[]{:S(2)}) collective-permute-start(f32[128,128]{1,0:T(8,128)S(1)} %get-tuple-element.19), channel_id=1, source_target_pairs={{1,0},{2,1},{3,2},{4,3},{5,4},{6,5},{7,6},{8,7},{9,8},{10,9},{11,1... | collective-permute-start | bytes 196616 | tf_op jit(solution)/shard_map/ppermute | solution.py:30
  389.4 0.7 copy-start.1
  396.6 49.3 %all-to-all-start.3 = ((f32[32,40,128]{2,1,0:T(8,128)}), f32[32,40,128]{2,1,0:T(8,128)}, u32[]{:S(2)}, u32[]{:S(2)}) async-start(f32[32,40,128]{2,1,0:T(8,128)} %bitcast.76), calls=%async_computation.3 | async-start | bytes 1310720 | tf_op jit(solution)/shard_map/all_to_all | solution.py:40
  401.7 197.0 %all-gather.14.cloned.1.call-start = ((), (), s32[]{:S(2)}) async-start(), calls=%async_computation.8 | async-start | bytes 5570560 | tf_op jit(solution)/shard_map/all_gather | solution.py:65
  402.7 24.6 %collective-permute-start.4 = (f32[128,128]{1,0:T(8,128)S(1)}, f32[128,128]{1,0:T(8,128)S(1)}, u32[]{:S(2)}, u32[]{:S(2)}) collective-permute-start(f32[128,128]{1,0:T(8,128)S(1)} %get-tuple-element.22), channel_id=1, source_target_pairs={{0,1},{1,2},{2,3},{3,4},{4,5},{5,6},{6,7},{7,8},{8,9},{9,10},{10,1... | collective-permute-start | bytes 196616 | tf_op jit(solution)/shard_map/ppermute | solution.py:21
  406.2 26.0 %collective-permute-start.5 = (f32[128,128]{1,0:T(8,128)S(1)}, f32[128,128]{1,0:T(8,128)S(1)}, u32[]{:S(2)}, u32[]{:S(2)}) collective-permute-start(f32[128,128]{1,0:T(8,128)S(1)} %get-tuple-element.23), channel_id=1, source_target_pairs={{1,0},{2,1},{3,2},{4,3},{5,4},{6,5},{7,6},{8,7},{9,8},{10,9},{11,1... | collective-permute-start | bytes 196616 | tf_op jit(solution)/shard_map/ppermute | solution.py:22
  559.2 46.3 %collective-permute-start.6 = (f32[128,128]{1,0:T(8,128)}, f32[128,128]{1,0:T(8,128)S(1)}, u32[]{:S(2)}, u32[]{:S(2)}) collective-permute-start(f32[128,128]{1,0:T(8,128)} %get-tuple-element.16), channel_id=1, source_target_pairs={{0,1},{1,2},{2,3},{3,4},{4,5},{5,6},{6,7},{7,8},{8,9},{9,10},{10,1... | collective-permute-start | bytes 196616 | tf_op jit(solution)/shard_map/ppermute | solution.py:30
  562.6 43.0 %collective-permute-start.7 = (f32[128,128]{1,0:T(8,128)S(1)}, f32[128,128]{1,0:T(8,128)S(1)}, u32[]{:S(2)}, u32[]{:S(2)}) collective-permute-start(f32[128,128]{1,0:T(8,128)S(1)} %get-tuple-element.17), channel_id=1, source_target_pairs={{1,0},{2,1},{3,2},{4,3},{5,4},{6,5},{7,6},{8,7},{9,8},{10,9},{11,1... | collective-permute-start | bytes 196616 | tf_op jit(solution)/shard_map/ppermute | solution.py:30
  633.5 0.7 copy-start.2
  640.7 48.6 %all-to-all-start.5 = ((f32[32,40,128]{2,1,0:T(8,128)}), f32[32,40,128]{2,1,0:T(8,128)}, u32[]{:S(2)}, u32[]{:S(2)}) async-start(f32[32,40,128]{2,1,0:T(8,128)} %bitcast.77), calls=%async_computation.5 | async-start | bytes 1310720 | tf_op jit(solution)/shard_map/all_to_all | solution.py:40
  646.7 24.7 %collective-permute-start.8 = (f32[128,128]{1,0:T(8,128)S(1)}, f32[128,128]{1,0:T(8,128)S(1)}, u32[]{:S(2)}, u32[]{:S(2)}) collective-permute-start(f32[128,128]{1,0:T(8,128)S(1)} %get-tuple-element.20), channel_id=1, source_target_pairs={{0,1},{1,2},{2,3},{3,4},{4,5},{5,6},{6,7},{7,8},{8,9},{9,10},{10,1... | collective-permute-start | bytes 196616 | tf_op jit(solution)/shard_map/ppermute | solution.py:21
  650.3 26.1 %collective-permute-start.9 = (f32[128,128]{1,0:T(8,128)S(1)}, f32[128,128]{1,0:T(8,128)S(1)}, u32[]{:S(2)}, u32[]{:S(2)}) collective-permute-start(f32[128,128]{1,0:T(8,128)S(1)} %get-tuple-element.21), channel_id=1, source_target_pairs={{1,0},{2,1},{3,2},{4,3},{5,4},{6,5},{7,6},{8,7},{9,8},{10,9},{11,1... | collective-permute-start | bytes 196616 | tf_op jit(solution)/shard_map/ppermute | solution.py:22
Sparse Core Ops, SparseCore 0:
  51.4 66.9 all-gather.9
  289.5 65.0 all-gather.11
  533.6 65.1 all-gather.13
where the time goes:
time: 762 us; the launch traced here: 752 us
  blocking collectives  309 us (41%)
  waiting for transfers between devices  211 us (28%)
  other arithmetic  74.5 us (10%)
  local copies, waits for them, and re-layouts  61.7 us (8%)
  starting transfers between devices  58.7 us (8%)
  matrix products  22.9 us (3%)
  between operations  13.9 us (2%)
    psum x12, blocking collectives, over_axes_2(): shard = lax.psum(shard, axis)  157 us
    all_gather x3, waiting for transfers between devices, total_of_pieces(): pieces = lax.all_gather(shard, axis)  137 us
    all_gather x6, blocking collectives, all_blocks(): pieces = lax.all_gather(pieces, axes[k], axis=0, tiled=True)  102 us
    ppermute x3, waiting for transfers between devices, extended_2(): before = lax.ppermute(last, axis, up)  55.1 us
    all_to_all x2, blocking collectives, sent_to_all(): lax.all_to_all(jnp.broadcast_to(shard[None], (length, *shard.shape)), axi...  49.6 us
    scatter-add x6, other arithmetic, shards(): spread = spread.at[local_ids[slot]].add(reg_resid)  45 us
    all_to_all x3, starting transfers between devices, summed_on_arrival(): lax.all_to_all(cut_along(shard, dim, length), axis, 0, 0, tiled=True)  18.1 us
  transfers between devices with their start and end apart: 17, of which 10 were waited for; matrix products, arithmetic and copies ran while one was open for 15% of the time, Pallas kernels for 0%

commit v1 on v0

--- a/solution.py
+++ b/solution.py
@@ -9,6 +9,11 @@
 PATCH = ("patch_0", "patch_1")
 OBS = ("obs_0", "obs_1")
 OBS_PATCH = ("obs_0", "obs_1", "patch_0", "patch_1")
+
+
+def all_by_exchange(block, name, dim):
+    outgoing = jnp.stack([block] * lax.axis_size(name))
+    return jnp.concatenate(lax.all_to_all(outgoing, name, 0, 0), axis=dim)
 
 
 def extended_2(shard, sides, width):
@@ -50,7 +55,7 @@
 def all_blocks(shard, axes, sequence):
     pieces = shard[None]
     for k in sequence:
-        pieces = lax.all_gather(pieces, axes[k], axis=0, tiled=True)
+        pieces = all_by_exchange(pieces, axes[k], 0)
     block = [lax.axis_size(axes[k]) for k in reversed(sequence)]
     pieces = pieces.reshape(*block, *shard.shape)
     turned = sorted(range(len(sequence)), key=lambda place: sequence[len(sequence) - 1 - place])

time: 762 us -> 764 us (level)
  blocking collectives: 309 us -> 318 us
    all_to_all x0 -> x6, blocking collectives: none -> 111 us  [all_by_exchange(): return jnp.concatenate(lax.all_to_all(outgoing, name, 0, 0), axis=dim)]
    all_gather x6 -> x0, blocking collectives: 102 us -> none  [all_blocks(): pieces = lax.all_gather(pieces, axes[k], axis=0, tiled=True)]
where the time goes in v1:
time: 764 us; the launch traced here: 753 us
  blocking collectives  318 us (42%)
  waiting for transfers between devices  204 us (27%)
  other arithmetic  74.7 us (10%)
  local copies, waits for them, and re-layouts  61.7 us (8%)
  starting transfers between devices  58.1 us (8%)
  matrix products  22.9 us (3%)
  between operations  13.6 us (2%)
    psum x12, blocking collectives, over_axes_2(): shard = lax.psum(shard, axis)  157 us
    all_gather x3, waiting for transfers between devices, total_of_pieces(): pieces = lax.all_gather(shard, axis)  130 us
    all_to_all x6, blocking collectives, all_by_exchange(): return jnp.concatenate(lax.all_to_all(outgoing, name, 0, 0), axis=dim)  111 us
    ppermute x3, waiting for transfers between devices, extended_2(): before = lax.ppermute(last, axis, up)  55.1 us
    all_to_all x2, blocking collectives, sent_to_all(): lax.all_to_all(jnp.broadcast_to(shard[None], (length, *shard.shape)), axi...  49.6 us
    scatter-add x6, other arithmetic, shards(): spread = spread.at[local_ids[slot]].add(reg_resid)  45.1 us
    all_to_all x3, starting transfers between devices, summed_on_arrival(): lax.all_to_all(cut_along(shard, dim, length), axis, 0, 0, tiled=True)  18.1 us
  transfers between devices with their start and end apart: 17, of which 10 were waited for; matrix products, arithmetic and copies ran while one was open for 15% of the time, Pallas kernels for 0%

profile of v1, /device:TPU:1, one launch (start us, length us, event | category | flops | bytes accessed | tf_op | source)
XLA Modules:
  0.0 753.3 jit_solution(1170588523259111757)
XLA Ops:
  7.4 31.0 %all_to_all.63 = f32[16,1,40,128]{3,2,1,0:T(8,128)S(1)} all-to-all(f32[16,1,40,128]{3,2,1,0:T(8,128)S(1)} %stack.18), channel_id=1, replica_groups=mesh['obs_0'=4,'obs_1'=4,'patch_0'=16,'patch_1'=2] {'patch_0'}, dimensions={0} | all-to-all | bytes 655360 | tf_op jit(solution)/shard_map/all_to_all | solution.py:16
  38.5 10.4 %all_to_all.64 = f32[2,16,40,128]{3,2,1,0:T(8,128)S(1)} all-to-all(f32[2,16,40,128]{3,2,1,0:T(8,128)S(1)} %pad_maximum_fusion), channel_id=1, replica_groups=mesh['obs_0'=4,'obs_1'=4,'patch_0'=16,'patch_1'=2] {'patch_1'}, dimensions={0} | all-to-all | bytes 1310720 | tf_op jit(solution)/shard_map/all_to_all | solution.py:16
  52.0 66.5 %all-gather.7.cloned.1.call-done = f32[10240,128]{0,1:T(8,128)} async-done(((f32[640,128]{0,1:T(8,128)}), f32[10240,128]{0,1:T(8,128)}) %all-gather.7.cloned.1.call-update) | async-done | bytes 5242896 | tf_op jit(solution)/shard_map/all_gather | solution.py:70
  118.4 3.4 copy.53
  124.2 13.2 %all-to-all-start.2 = ((f32[32,1,128]{2,1,0:T(1,128)}), f32[32,1,128]{2,1,0:T(1,128)S(1)}, u32[]{:S(2)}, u32[]{:S(2)}) async-start(f32[32,1,128]{2,1,0:T(1,128)} %broadcast_in_dim.14), calls=%async_computation.2 | async-start | bytes 32768 | tf_op jit(solution)/shard_map/all_to_all | solution.py:76
  137.4 5.3 convolution_bitcast_fusion.2
  144.8 4.3 all-to-all-done.2
  149.1 7.9 %all-to-all-start.3 = ((f32[32,40,128]{2,1,0:T(8,128)}), f32[32,40,128]{2,1,0:T(8,128)}, u32[]{:S(2)}, u32[]{:S(2)}) async-start(f32[32,40,128]{2,1,0:T(8,128)} %bitcast.72), calls=%async_computation.3 | async-start | bytes 1310720 | tf_op jit(solution)/shard_map/all_to_all | solution.py:45
  160.6 3.5 collective-permute-start
  166.0 16.8 %collective-permute-done = f32[128,128]{1,0:T(8,128)S(1)} collective-permute-done((f32[128,128]{1,0:T(8,128)}, f32[128,128]{1,0:T(8,128)S(1)}, u32[]{:S(2)}, u32[]{:S(2)}) %collective-permute-start) | collective-permute-done | bytes 65568 | tf_op jit(solution)/shard_map/ppermute | solution.py:26
  182.8 4.5 collective-permute-done.1
  202.1 8.4 %psum.84 = f32[128]{0:T(128)S(1)} all-reduce(f32[128]{0:T(128)S(1)} %fusion.23), channel_id=1, replica_groups=mesh['obs_0'=4,'obs_1'=4,'patch_0'=16,'patch_1'=2] {'obs_0'}, use_global_device_ids=true, to_apply=%region_6.7 | all-reduce | flops 128 | bytes 1024 | tf_op jit(solution)/shard_map/psum | solution.py:88
  210.5 6.5 psum.85
  217.1 24.1 %psum.86 = f32[128]{0:T(128)S(1)} all-reduce(f32[128]{0:T(128)S(1)} %psum.85), channel_id=1, replica_groups=mesh['obs_0'=4,'obs_1'=4,'patch_0'=16,'patch_1'=2] {'patch_0'}, use_global_device_ids=true, to_apply=%region_8.9 | all-reduce | flops 128 | bytes 1024 | tf_op jit(solution)/shard_map/psum | solution.py:88
  241.2 13.6 %psum.87 = f32[128]{0:T(128)S(1)} all-reduce(f32[128]{0:T(128)S(1)} %psum.86), channel_id=1, replica_groups=mesh['obs_0'=4,'obs_1'=4,'patch_0'=16,'patch_1'=2] {'patch_1'}, use_global_device_ids=true, to_apply=%region_9.10 | all-reduce | flops 128 | bytes 1024 | tf_op jit(solution)/shard_map/psum | solution.py:88
  255.5 24.2 %all_to_all.65 = f32[16,1,40,128]{3,2,1,0:T(8,128)S(1)} all-to-all(f32[16,1,40,128]{3,2,1,0:T(8,128)S(1)} %stack.20), channel_id=1, replica_groups=mesh['obs_0'=4,'obs_1'=4,'patch_0'=16,'patch_1'=2] {'patch_0'}, dimensions={0} | all-to-all | bytes 655360 | tf_op jit(solution)/shard_map/all_to_all | solution.py:16
  279.8 10.6 %all_to_all.66 = f32[2,16,40,128]{3,2,1,0:T(8,128)S(1)} all-to-all(f32[2,16,40,128]{3,2,1,0:T(8,128)S(1)} %pad_maximum_fusion.1), channel_id=1, replica_groups=mesh['obs_0'=4,'obs_1'=4,'patch_0'=16,'patch_1'=2] {'patch_1'}, dimensions={0} | all-to-all | bytes 1310720 | tf_op jit(solution)/shard_map/all_to_all | solution.py:16
  293.4 7.2 scatter_custom_fusion
  300.7 7.7 %scatter_custom_fusion.1 = f32[896,128]{1,0:T(8,128)} fusion(f32[896,128]{1,0:T(8,128)} %scatter_custom_fusion, s32[640]{0:T(1024)S(1)} %get-tuple-element.7, f32[640,128]{1,0:T(8,128)} %get-tuple-element.15, f32[]{:T(128)} %constant.8.clone.1, f32[128]{0:T(128)S(1)} %div.23), kind=kCustom, calls=%fused_computation.58 | custom fusion | flops 245760 | bytes 787456 | tf_op jit(solution)/shard_map/scatter-add | solution.py:150
  308.4 7.7 %scatter_custom_fusion.2 = f32[896,128]{1,0:T(8,128)} fusion(f32[896,128]{1,0:T(8,128)} %scatter_custom_fusion.1, s32[640]{0:T(1024)S(1)} %get-tuple-element.6, f32[640,128]{1,0:T(8,128)} %get-tuple-element.15, f32[]{:T(128)} %constant.8.clone.1, f32[128]{0:T(128)S(1)} %div.23), kind=kCustom, calls=%fused_computation.57 | custom fusion | flops 245760 | bytes 787456 | tf_op jit(solution)/shard_map/scatter-add | solution.py:150
  322.6 33.0 %all-gather.9.cloned.1.call-done = f32[10240,128]{0,1:T(8,128)} async-done(((f32[640,128]{0,1:T(8,128)}), f32[10240,128]{0,1:T(8,128)}) %all-gather.9.cloned.1.call-update) | async-done | bytes 5242896 | tf_op jit(solution)/shard_map/all_gather | solution.py:70
  355.5 3.4 copy.54
  364.4 24.8 %all_to_all.67 = f32[32,1,128]{2,1,0:T(1,128)S(1)} all-to-all(f32[32,1,128]{2,1,0:T(1,128)S(1)} %broadcast_in_dim.17), channel_id=1, replica_groups=mesh['obs_0'=4,'obs_1'=4,'patch_0'=16,'patch_1'=2] {'patch_0','patch_1'}, dimensions={0} | all-to-all | bytes 32768 | tf_op jit(solution)/shard_map/all_to_all | solution.py:76
  391.1 4.3 convolution_bitcast_fusion.1
  397.5 5.1 all-to-all-start.7
  403.6 3.5 collective-permute-start.4
  409.1 19.1 %collective-permute-done.4 = f32[128,128]{1,0:T(8,128)S(1)} collective-permute-done((f32[128,128]{1,0:T(8,128)S(1)}, f32[128,128]{1,0:T(8,128)S(1)}, u32[]{:S(2)}, u32[]{:S(2)}) %collective-permute-start.4) | collective-permute-done | bytes 65568 | tf_op jit(solution)/shard_map/ppermute | solution.py:26
  428.2 5.0 collective-permute-done.5
  448.0 8.4 %psum.88 = f32[128]{0:T(128)S(1)} all-reduce(f32[128]{0:T(128)S(1)} %fusion.24), channel_id=1, replica_groups=mesh['obs_0'=4,'obs_1'=4,'patch_0'=16,'patch_1'=2] {'obs_0'}, use_global_device_ids=true, to_apply=%region_19.20 | all-reduce | flops 128 | bytes 1024 | tf_op jit(solution)/shard_map/psum | solution.py:88
  456.4 6.5 psum.89
  463.0 23.9 %psum.90 = f32[128]{0:T(128)S(1)} all-reduce(f32[128]{0:T(128)S(1)} %psum.89), channel_id=1, replica_groups=mesh['obs_0'=4,'obs_1'=4,'patch_0'=16,'patch_1'=2] {'patch_0'}, use_global_device_ids=true, to_apply=%region_21.22 | all-reduce | flops 128 | bytes 1024 | tf_op jit(solution)/shard_map/psum | solution.py:88
  486.8 13.6 %psum.91 = f32[128]{0:T(128)S(1)} all-reduce(f32[128]{0:T(128)S(1)} %psum.90), channel_id=1, replica_groups=mesh['obs_0'=4,'obs_1'=4,'patch_0'=16,'patch_1'=2] {'patch_1'}, use_global_device_ids=true, to_apply=%region_22.23 | all-reduce | flops 128 | bytes 1024 | tf_op jit(solution)/shard_map/psum | solution.py:88
  500.5 24.2 %all_to_all.68 = f32[16,1,40,128]{3,2,1,0:T(8,128)S(1)} all-to-all(f32[16,1,40,128]{3,2,1,0:T(8,128)S(1)} %stack.22), channel_id=1, replica_groups=mesh['obs_0'=4,'obs_1'=4,'patch_0'=16,'patch_1'=2] {'patch_0'}, dimensions={0} | all-to-all | bytes 655360 | tf_op jit(solution)/shard_map/all_to_all | solution.py:16
  524.7 10.6 %all_to_all.69 = f32[2,16,40,128]{3,2,1,0:T(8,128)S(1)} all-to-all(f32[2,16,40,128]{3,2,1,0:T(8,128)S(1)} %pad_maximum_fusion.2), channel_id=1, replica_groups=mesh['obs_0'=4,'obs_1'=4,'patch_0'=16,'patch_1'=2] {'patch_1'}, dimensions={0} | all-to-all | bytes 1310720 | tf_op jit(solution)/shard_map/all_to_all | solution.py:16
  540.3 7.2 scatter_custom_fusion.3
  547.5 7.7 %scatter_fusion = f32[896,128]{1,0:T(8,128)} fusion(f32[896,128]{1,0:T(8,128)} %scatter_custom_fusion.3, s32[640]{0:T(1024)S(1)} %get-tuple-element.7, f32[640,128]{1,0:T(8,128)} %multiply_subtract_fusion), kind=kCustom, calls=%fused_computation.13 | custom fusion | flops 81920 | bytes 985600 | tf_op jit(solution)/shard_map/scatter-add | solution.py:150
  555.2 7.6 %scatter_fusion.1 = f32[896,128]{1,0:T(8,128)} fusion(f32[896,128]{1,0:T(8,128)} %scatter_fusion, s32[640]{0:T(1024)S(1)} %get-tuple-element.6, f32[640,128]{1,0:T(8,128)} %multiply_subtract_fusion), kind=kCustom, calls=%fused_computation.14 | custom fusion | flops 81920 | bytes 985600 | tf_op jit(solution)/shard_map/scatter-add | solution.py:150
  569.6 31.0 %all-gather.11.cloned.1.call-done = f32[10240,128]{0,1:T(8,128)} async-done(((f32[640,128]{0,1:T(8,128)}), f32[10240,128]{0,1:T(8,128)}) %all-gather.11.cloned.1.call-update) | async-done | bytes 5242896 | tf_op jit(solution)/shard_map/all_gather | solution.py:70
  609.4 24.8 %all_to_all.70 = f32[32,1,128]{2,1,0:T(1,128)S(1)} all-to-all(f32[32,1,128]{2,1,0:T(1,128)S(1)} %broadcast_in_dim.18), channel_id=1, replica_groups=mesh['obs_0'=4,'obs_1'=4,'patch_0'=16,'patch_1'=2] {'patch_0','patch_1'}, dimensions={0} | all-to-all | bytes 32768 | tf_op jit(solution)/shard_map/all_to_all | solution.py:76
  636.1 4.3 convolution_bitcast_fusion
  642.5 5.1 all-to-all-start.11
  648.5 3.5 collective-permute-start.8
  654.0 19.2 %collective-permute-done.8 = f32[128,128]{1,0:T(8,128)S(1)} collective-permute-done((f32[128,128]{1,0:T(8,128)S(1)}, f32[128,128]{1,0:T(8,128)S(1)}, u32[]{:S(2)}, u32[]{:S(2)}) %collective-permute-start.8) | collective-permute-done | bytes 65568 | tf_op jit(solution)/shard_map/ppermute | solution.py:26
  673.2 5.0 collective-permute-done.9
  692.3 8.4 %psum.92 = f32[128]{0:T(128)S(1)} all-reduce(f32[128]{0:T(128)S(1)} %fusion.25), channel_id=1, replica_groups=mesh['obs_0'=4,'obs_1'=4,'patch_0'=16,'patch_1'=2] {'obs_0'}, use_global_device_ids=true, to_apply=%region_32.33 | all-reduce | flops 128 | bytes 1024 | tf_op jit(solution)/shard_map/psum | solution.py:88
  700.7 6.8 psum.93
  707.5 23.7 %psum.94 = f32[128]{0:T(128)S(1)} all-reduce(f32[128]{0:T(128)S(1)} %psum.93), channel_id=1, replica_groups=mesh['obs_0'=4,'obs_1'=4,'patch_0'=16,'patch_1'=2] {'patch_0'}, use_global_device_ids=true, to_apply=%region_34.35 | all-reduce | flops 128 | bytes 1024 | tf_op jit(solution)/shard_map/psum | solution.py:88
  731.1 13.6 %psum.95 = f32[128]{0:T(128)S(1)} all-reduce(f32[128]{0:T(128)S(1)} %psum.94), channel_id=1, replica_groups=mesh['obs_0'=4,'obs_1'=4,'patch_0'=16,'patch_1'=2] {'patch_1'}, use_global_device_ids=true, to_apply=%region_35.36 | all-reduce | flops 128 | bytes 1024 | tf_op jit(solution)/shard_map/psum | solution.py:88
  (108 shorter events, 109.8 us)
Async XLA Ops:
  6.5 42.4 %copy-start = (f32[1280,640]{1,0:T(8,128)S(1)}, f32[1280,640]{1,0:T(8,128)}, u32[]{:S(2)}) copy-start(f32[1280,640]{1,0:T(8,128)} %param.4) | copy-start | bytes 9830404
  6.5 111.9 %all-gather.7.cloned.1.call-start = ((), (), s32[]{:S(2)}) async-start(), calls=%async_computation.12 | async-start | bytes 5570560 | tf_op jit(solution)/shard_map/all_gather | solution.py:70
  122.7 0.7 copy-start.3
  124.2 24.9 %all-to-all-start.2 = ((f32[32,1,128]{2,1,0:T(1,128)}), f32[32,1,128]{2,1,0:T(1,128)S(1)}, u32[]{:S(2)}, u32[]{:S(2)}) async-start(f32[32,1,128]{2,1,0:T(1,128)} %broadcast_in_dim.14), calls=%async_computation.2 | async-start | bytes 32768 | tf_op jit(solution)/shard_map/all_to_all | solution.py:76
  137.4 19.7 %copy-start.5 = (s32[3,640]{1,0:T(4,128)S(1)}, s32[3,640]{1,0:T(4,128)}, u32[]{:S(2)}) copy-start(s32[3,640]{1,0:T(4,128)} %param.6) | copy-start | bytes 23044
  149.1 51.8 %all-to-all-start.3 = ((f32[32,40,128]{2,1,0:T(8,128)}), f32[32,40,128]{2,1,0:T(8,128)}, u32[]{:S(2)}, u32[]{:S(2)}) async-start(f32[32,40,128]{2,1,0:T(8,128)} %bitcast.72), calls=%async_computation.3 | async-start | bytes 1310720 | tf_op jit(solution)/shard_map/all_to_all | solution.py:45
  157.0 198.5 %all-gather.9.cloned.1.call-start = ((), (), s32[]{:S(2)}) async-start(), calls=%async_computation.13 | async-start | bytes 5570560 | tf_op jit(solution)/shard_map/all_gather | solution.py:70
  160.6 22.3 %collective-permute-start = (f32[128,128]{1,0:T(8,128)}, f32[128,128]{1,0:T(8,128)S(1)}, u32[]{:S(2)}, u32[]{:S(2)}) collective-permute-start(f32[128,128]{1,0:T(8,128)} %get-tuple-element.24), channel_id=1, source_target_pairs={{0,1},{1,2},{2,3},{3,4},{4,5},{5,6},{6,7},{7,8},{8,9},{9,10},{10,1... | collective-permute-start | bytes 196616 | tf_op jit(solution)/shard_map/ppermute | solution.py:26
  164.1 23.2 %collective-permute-start.1 = (f32[128,128]{1,0:T(8,128)S(1)}, f32[128,128]{1,0:T(8,128)S(1)}, u32[]{:S(2)}, u32[]{:S(2)}) collective-permute-start(f32[128,128]{1,0:T(8,128)S(1)} %get-tuple-element.25), channel_id=1, source_target_pairs={{1,0},{2,1},{3,2},{4,3},{5,4},{6,5},{7,6},{8,7},{9,8},{10,9},{11,1... | collective-permute-start | bytes 196616 | tf_op jit(solution)/shard_map/ppermute | solution.py:27
  192.3 6.5 copy-start.4
  317.5 44.9 %collective-permute-start.2 = (f32[128,128]{1,0:T(8,128)}, f32[128,128]{1,0:T(8,128)S(1)}, u32[]{:S(2)}, u32[]{:S(2)}) collective-permute-start(f32[128,128]{1,0:T(8,128)} %get-tuple-element.18), channel_id=1, source_target_pairs={{0,1},{1,2},{2,3},{3,4},{4,5},{5,6},{6,7},{7,8},{8,9},{9,10},{10,1... | collective-permute-start | bytes 196616 | tf_op jit(solution)/shard_map/ppermute | solution.py:35
  320.5 41.9 %collective-permute-start.3 = (f32[128,128]{1,0:T(8,128)S(1)}, f32[128,128]{1,0:T(8,128)S(1)}, u32[]{:S(2)}, u32[]{:S(2)}) collective-permute-start(f32[128,128]{1,0:T(8,128)S(1)} %get-tuple-element.19), channel_id=1, source_target_pairs={{1,0},{2,1},{3,2},{4,3},{5,4},{6,5},{7,6},{8,7},{9,8},{10,9},{11,1... | collective-permute-start | bytes 196616 | tf_op jit(solution)/shard_map/ppermute | solution.py:35
  390.3 0.7 copy-start.1
  397.5 49.3 %all-to-all-start.7 = ((f32[32,40,128]{2,1,0:T(8,128)}), f32[32,40,128]{2,1,0:T(8,128)}, u32[]{:S(2)}, u32[]{:S(2)}) async-start(f32[32,40,128]{2,1,0:T(8,128)} %bitcast.73), calls=%async_computation.7 | async-start | bytes 1310720 | tf_op jit(solution)/shard_map/all_to_all | solution.py:45
  402.7 197.9 %all-gather.11.cloned.1.call-start = ((), (), s32[]{:S(2)}) async-start(), calls=%async_computation.14 | async-start | bytes 5570560 | tf_op jit(solution)/shard_map/all_gather | solution.py:70
  403.6 24.6 %collective-permute-start.4 = (f32[128,128]{1,0:T(8,128)S(1)}, f32[128,128]{1,0:T(8,128)S(1)}, u32[]{:S(2)}, u32[]{:S(2)}) collective-permute-start(f32[128,128]{1,0:T(8,128)S(1)} %get-tuple-element.22), channel_id=1, source_target_pairs={{0,1},{1,2},{2,3},{3,4},{4,5},{5,6},{6,7},{7,8},{8,9},{9,10},{10,1... | collective-permute-start | bytes 196616 | tf_op jit(solution)/shard_map/ppermute | solution.py:26
  407.1 26.0 %collective-permute-start.5 = (f32[128,128]{1,0:T(8,128)S(1)}, f32[128,128]{1,0:T(8,128)S(1)}, u32[]{:S(2)}, u32[]{:S(2)}) collective-permute-start(f32[128,128]{1,0:T(8,128)S(1)} %get-tuple-element.23), channel_id=1, source_target_pairs={{1,0},{2,1},{3,2},{4,3},{5,4},{6,5},{7,6},{8,7},{9,8},{10,9},{11,1... | collective-permute-start | bytes 196616 | tf_op jit(solution)/shard_map/ppermute | solution.py:27
  564.3 43.1 %collective-permute-start.6 = (f32[128,128]{1,0:T(8,128)}, f32[128,128]{1,0:T(8,128)S(1)}, u32[]{:S(2)}, u32[]{:S(2)}) collective-permute-start(f32[128,128]{1,0:T(8,128)} %get-tuple-element.16), channel_id=1, source_target_pairs={{0,1},{1,2},{2,3},{3,4},{4,5},{5,6},{6,7},{7,8},{8,9},{9,10},{10,1... | collective-permute-start | bytes 196616 | tf_op jit(solution)/shard_map/ppermute | solution.py:35
  567.2 40.2 %collective-permute-start.7 = (f32[128,128]{1,0:T(8,128)S(1)}, f32[128,128]{1,0:T(8,128)S(1)}, u32[]{:S(2)}, u32[]{:S(2)}) collective-permute-start(f32[128,128]{1,0:T(8,128)S(1)} %get-tuple-element.17), channel_id=1, source_target_pairs={{1,0},{2,1},{3,2},{4,3},{5,4},{6,5},{7,6},{8,7},{9,8},{10,9},{11,1... | collective-permute-start | bytes 196616 | tf_op jit(solution)/shard_map/ppermute | solution.py:35
  635.3 0.7 copy-start.2
  642.5 48.6 %all-to-all-start.11 = ((f32[32,40,128]{2,1,0:T(8,128)}), f32[32,40,128]{2,1,0:T(8,128)}, u32[]{:S(2)}, u32[]{:S(2)}) async-start(f32[32,40,128]{2,1,0:T(8,128)} %bitcast.74), calls=%async_computation.11 | async-start | bytes 1310720 | tf_op jit(solution)/shard_map/all_to_all | solution.py:45
  648.5 24.7 %collective-permute-start.8 = (f32[128,128]{1,0:T(8,128)S(1)}, f32[128,128]{1,0:T(8,128)S(1)}, u32[]{:S(2)}, u32[]{:S(2)}) collective-permute-start(f32[128,128]{1,0:T(8,128)S(1)} %get-tuple-element.20), channel_id=1, source_target_pairs={{0,1},{1,2},{2,3},{3,4},{4,5},{5,6},{6,7},{7,8},{8,9},{9,10},{10,1... | collective-permute-start | bytes 196616 | tf_op jit(solution)/shard_map/ppermute | solution.py:26
  652.1 26.1 %collective-permute-start.9 = (f32[128,128]{1,0:T(8,128)S(1)}, f32[128,128]{1,0:T(8,128)S(1)}, u32[]{:S(2)}, u32[]{:S(2)}) collective-permute-start(f32[128,128]{1,0:T(8,128)S(1)} %get-tuple-element.21), channel_id=1, source_target_pairs={{1,0},{2,1},{3,2},{4,3},{5,4},{6,5},{7,6},{8,7},{9,8},{10,9},{11,1... | collective-permute-start | bytes 196616 | tf_op jit(solution)/shard_map/ppermute | solution.py:27
Sparse Core Ops, SparseCore 0:
  52.1 66.3 all-gather.6
  293.6 61.9 all-gather.8
  538.6 61.9 all-gather.10
